TPU v7x, 32 devices: a whole 2x2x4 slice. The times are simulated.
32 devices in a mesh: rows: 8 (over z, y), mem: 4 (over x, core).
Axes of the slice: x: 2, y: 2, z: 4, core: 2. Of those that a mesh axis runs over, the one named last changes fastest.
Arguments:
- ensemble: float32 [64, 32, 48, 384], P('mem', None, 'rows'), may hold values from 0 to 2
- courant: float32 [3, 32, 48, 384], P(None, None, 'rows'), may hold values from -0.22 to 0.22
- obs_column: int32 [128], P('rows'), may hold values from 0 to 18431, as said below
- obs_value: float32 [32, 128], P(None, 'rows'), may hold values from -6 to 6
- obs_var: float32 [32, 128], P(None, 'rows'), may hold values from 0.5 to 8
Outputs:
- analysis: float32 [64, 32, 48, 384], P('mem', None, 'rows')
Inputs may be any that keep to these rules, and one draw needn't show every extreme that they name: `obs_column`: entry p is x * 384 + y with x from (p // 16) * 6 to (p // 16) * 6 + 5.
All inputs are finite; a program needn't handle non-finite values.
Results may differ from a plain program's by a relative error of at most 0.0003.
Values sent between devices are 32-bit elements; how exact they have to be, the bound alone decides.
A program may use at most 128 MiB of HBM per device.

v0:
```python
import functools

import jax
import jax.numpy as jnp
from jax import lax
from jax.experimental import pallas as pl
from jax.experimental.pallas import tpu as pltpu
from jax.sharding import PartitionSpec as P

STEPS = 3
NS_ITERS = 4
DIFFUSION = 0.05
AHEAD = 2
LANES = 128
MESH = pl.DeviceIdType.MESH
HIGHEST = lax.Precision.HIGHEST


def kernel(
    rows_n, mem_n,
    ens, cour, obs_x, obs_y, obs_value, obs_var,
    out,
    chalo, hal, coef, w0, w1, w2, w3, fc, st, prof, grec, wts,
    c_send, c_recv, cf_send, cf_recv, h_send, h_recv,
    x_send, p_send, f_recv, q_send, q_recv, g_send, g_recv,
):
    members, rows, levels, width = ens.shape
    total = members * mem_n
    nobs = obs_x.shape[0]
    chips = mem_n // 2
    row = lax.axis_index("rows")
    mem = lax.axis_index("mem")
    core = lax.rem(mem, 2)
    chip = mem // 2
    partner = chip * 2 + 1 - core

    def dev(r, m):
        return {"rows": r, "mem": m}

    def remote(src, dst, ssem, rsem, r, m):
        return pltpu.make_async_remote_copy(
            src_ref=src, dst_ref=dst, send_sem=ssem, recv_sem=rsem,
            device_id=(r, m), device_id_type=MESH,
        )

    barrier = pltpu.get_barrier_semaphore()
    for d in range(1, mem_n):
        pl.semaphore_signal(barrier, inc=1, device_id=(row, lax.rem(mem + d, mem_n)), device_id_type=MESH)
    for d in range(1, rows_n):
        pl.semaphore_signal(barrier, inc=1, device_id=(lax.rem(row + d, rows_n), mem), device_id_type=MESH)
    pl.semaphore_wait(barrier, mem_n - 1 + rows_n - 1)

    has_low = row > 0
    has_high = row < rows_n - 1
    low = jnp.maximum(row - 1, 0)
    high = jnp.minimum(row + 1, rows_n - 1)

    def chalo_up():
        return remote(cour.at[:, rows - 2 + core], chalo.at[0, core], c_send.at[0], c_recv.at[0], high, mem)

    def chalo_down():
        return remote(cour.at[:, core], chalo.at[1, core], c_send.at[1], c_recv.at[1], low, mem)

    def chalo_pass(side):
        return remote(chalo.at[side, core], chalo.at[side, core], cf_send.at[side], cf_recv.at[side], row, partner)

    def halo_up(m):
        return remote(ens.at[m, pl.ds(rows - 3, 3)], hal.at[m, 0], h_send.at[0, m], h_recv.at[0, m], high, mem)

    def halo_down(m):
        return remote(ens.at[m, pl.ds(0, 3)], hal.at[m, 1], h_send.at[1, m], h_recv.at[1, m], low, mem)

    @pl.when(has_high)
    def _():
        chalo_up().start()

    @pl.when(has_low)
    def _():
        chalo_down().start()

    def send_halo(m):
        @pl.when(has_high)
        def _():
            halo_up(m).start()

        @pl.when(has_low)
        def _():
            halo_down(m).start()

    ahead = min(AHEAD, members)

    @pl.loop(0, ahead)
    def _(m):
        send_halo(m)

    level = lax.broadcasted_iota(jnp.int32, (levels, width), 0)
    cell = lax.broadcasted_iota(jnp.int32, (levels, width), 1)

    def set_coef(i, a0, a1, a2):
        coef[i, 0] = 1.0 - 6.0 * DIFFUSION - jnp.abs(a0) - jnp.abs(a1) - jnp.abs(a2)
        coef[i, 1] = DIFFUSION + jnp.maximum(a0, 0.0)
        coef[i, 2] = DIFFUSION - jnp.minimum(a0, 0.0)
        coef[i, 3] = jnp.where(cell > 0, DIFFUSION + jnp.maximum(a1, 0.0), 0.0)
        coef[i, 4] = jnp.where(cell < width - 1, DIFFUSION - jnp.minimum(a1, 0.0), 0.0)
        coef[i, 5] = jnp.where(level > 0, DIFFUSION + jnp.maximum(a2, 0.0), 0.0)
        coef[i, 6] = jnp.where(level < levels - 1, DIFFUSION - jnp.minimum(a2, 0.0), 0.0)

    @pl.loop(0, rows)
    def _(i):
        set_coef(i + 2, cour[0, i], cour[1, i], cour[2, i])

    st[...] = jnp.zeros_like(st)

    def edge(side, present, first):
        @pl.when(present)
        def _():
            (chalo_down if side else chalo_up)().wait_recv()
            chalo_pass(side).start()
            chalo_pass(side).wait_recv()

            @pl.loop(0, 2)
            def _(i):
                set_coef(first + i, chalo[side, i, 0], chalo[side, i, 1], chalo[side, i, 2])

        @pl.when(jnp.logical_not(present))
        def _():
            coef[pl.ds(first, 2)] = jnp.zeros((2, 7, levels, width), jnp.float32)

    edge(0, has_low, 0)
    edge(1, has_high, rows + 2)

    @pl.when(jnp.logical_not(has_low))
    def _():
        w0[pl.ds(0, 3)] = jnp.zeros((3, levels, width), jnp.float32)

    @pl.when(jnp.logical_not(has_high))
    def _():
        w0[pl.ds(rows + 3, 3)] = jnp.zeros((3, levels, width), jnp.float32)

    def update(src, i, c):
        mid = src[i + 1]
        return (
            coef[c, 0] * mid
            + coef[c, 1] * src[i]
            + coef[c, 2] * src[i + 2]
            + coef[c, 3] * pltpu.roll(mid, 1, 1)
            + coef[c, 4] * pltpu.roll(mid, width - 1, 1)
            + coef[c, 5] * pltpu.roll(mid, 1, 0)
            + coef[c, 6] * pltpu.roll(mid, levels - 1, 0)
        )

    def other(d):
        return lax.rem(chip + d, chips) * 2 + core

    def send_x(d, m):
        slot = fc.at[mem * members + m]
        return remote(slot, slot, x_send.at[d, m], f_recv.at[mem, m], row, other(d))

    def send_p(d, m):
        src = lax.rem(chip + d, chips) * 2 + core
        slot = fc.at[src * members + m]
        return remote(slot, slot, p_send.at[d, m], f_recv.at[src, m], row, partner)

    def arrived(src, m):
        slot = fc.at[src * members + m]
        return remote(slot, slot, p_send.at[0, 0], f_recv.at[src, m], row, partner)

    def forward(m):
        for d in range(1, chips):
            arrived(other(d), m).wait_recv()
            send_p(d, m).start()

    lane = lax.broadcasted_iota(jnp.int32, (levels, LANES), 1)
    lag = 2

    @pl.loop(0, members)
    def _(m):
        @pl.when(has_low)
        def _():
            halo_up(m).wait_recv()
            w0[pl.ds(0, 3)] = hal[m, 0]

        @pl.when(has_high)
        def _():
            halo_down(m).wait_recv()
            w0[pl.ds(rows + 3, 3)] = hal[m, 1]

        @pl.when(m + ahead < members)
        def _():
            send_halo(m + ahead)

        w0[pl.ds(3, rows)] = ens[m]

        @pl.loop(0, rows + 4, unroll=2)
        def _(i):
            w1[i] = update(w0, i, i)

        @pl.loop(0, rows + 2, unroll=2)
        def _(i):
            w2[i] = update(w1, i, i + 1)

        @pl.loop(0, rows, unroll=2)
        def _(i):
            value = update(w2, i, i + 2)
            w3[i] = value
            fc[mem * members + m, i] = value

        @pl.loop(0, nobs, unroll=4)
        def _(p):
            plane = w3[obs_x[p]]
            hit = cell == obs_y[p]
            picked = jnp.sum(jnp.where(hit, plane, 0.0), axis=1, keepdims=True)
            where = pl.ds(pl.multiple_of(p * levels, levels), levels)
            st[where] = jnp.where(lane == m, picked, st[where])

        for d in range(1, chips):
            send_x(d, m).start()
        send_p(0, m).start()

        @pl.when(m >= lag)
        def _():
            forward(m - lag)

    def dot(a, b):
        return jnp.dot(a, b, precision=HIGHEST, preferred_element_type=jnp.float32)

    def flat(ref):
        n = nobs * levels
        spread = lax.broadcasted_iota(jnp.int32, (levels, n), 1) % levels
        spread = jnp.where(spread == lax.broadcasted_iota(jnp.int32, (levels, n), 0), 1.0, 0.0)
        wide = dot(ref[...], spread.astype(jnp.float32))
        owner = lax.broadcasted_iota(jnp.int32, (nobs, n), 1) // levels
        own = owner == lax.broadcasted_iota(jnp.int32, (nobs, n), 0)
        return jnp.sum(jnp.where(own, wide, 0.0), axis=0, keepdims=True)

    mine = pl.ds(pl.multiple_of(mem * members, members), members)
    prof[mine] = st[...].T[:members]
    for d in range(1, mem_n):
        remote(prof.at[mine], prof.at[mine], q_send.at[d], q_recv.at[mem], row, lax.rem(mem + d, mem_n)).start()
    for d in range(1, mem_n):
        src = lax.rem(mem + d, mem_n)
        block = prof.at[pl.ds(pl.multiple_of(src * members, members), members)]
        remote(block, block, q_send.at[d], q_recv.at[src], row, src).wait_recv()

    values = prof[...]
    variance = flat(obs_var)
    center = jnp.mean(values, axis=0, keepdims=True)
    scaled = (values - center) / jnp.sqrt((total - 1.0) * variance)
    innovation = (flat(obs_value) - center) / jnp.sqrt(variance)
    pad = jnp.broadcast_to(innovation, (LANES - total, innovation.shape[1]))
    both = jnp.concatenate([scaled, pad], axis=0)
    grec[row] = lax.dot_general(
        scaled, both, (((1,), (1,)), ((), ())), precision=HIGHEST, preferred_element_type=jnp.float32
    )
    for d in range(1, rows_n):
        remote(grec.at[row], grec.at[row], g_send.at[d], g_recv.at[row], lax.rem(row + d, rows_n), mem).start()

    forward(members - 2)
    forward(members - 1)

    for d in range(1, rows_n):
        src = lax.rem(row + d, rows_n)
        remote(grec.at[src], grec.at[src], g_send.at[d], g_recv.at[src], src, mem).wait_recv()
    gsum = grec[0]
    for r in range(1, rows_n):
        gsum = gsum + grec[r]

    ri = lax.broadcasted_iota(jnp.int32, (total, total), 0)
    ci = lax.broadcasted_iota(jnp.int32, (total, total), 1)
    eye = jnp.where(ri == ci, 1.0, 0.0).astype(jnp.float32)
    system = eye + gsum[:, :total]
    frob = jnp.sqrt(jnp.sum(jnp.sum(system * system, axis=1, keepdims=True), axis=0, keepdims=True))
    y = system / frob
    z = eye
    for it in range(NS_ITERS):
        factor = 0.5 * (3.0 * eye - (y if it == 0 else dot(z, y)))
        if it < NS_ITERS - 1:
            y = dot(y, factor)
        z = factor if it == 0 else dot(factor, z)
    root = z / jnp.sqrt(frob)
    shift = dot(root, dot(root, gsum))[:, total:total + 1] / jnp.sqrt(jnp.float32(total - 1.0))
    mixed = shift + root
    weights = 1.0 / total + mixed - jnp.mean(mixed, axis=0, keepdims=True)
    wts[...] = weights.T
    tile = 8
    outs, ins = members * tile, total * tile

    def hot(shape, dim, size):
        big = lax.broadcasted_iota(jnp.int32, shape, dim) // size
        return jnp.where(big == lax.broadcasted_iota(jnp.int32, shape, 1 - dim), 1.0, 0.0).astype(jnp.float32)

    wide = dot(dot(hot((outs, members), 0, tile), wts[mine]), hot((total, ins), 1, tile))
    same = (
        lax.broadcasted_iota(jnp.int32, (outs, ins), 0) % tile
        == lax.broadcasted_iota(jnp.int32, (outs, ins), 1) % tile
    )
    wide = jnp.where(same, wide, 0.0)
    wide_high = wide.astype(jnp.bfloat16)
    wide_low = (wide - wide_high.astype(jnp.float32)).astype(jnp.bfloat16)

    for d in range(chips):
        src = lax.rem(chip + d, chips) * 2 + 1 - core

        @pl.loop(0, members)
        def _(m):
            arrived(src, m).wait_recv()

    def dot16(a, b):
        return jnp.dot(a, b, preferred_element_type=jnp.float32)

    @pl.loop(0, rows * (levels // tile), unroll=2)
    def _(n):
        i = n // (levels // tile)
        where = pl.ds(pl.multiple_of(lax.rem(n, levels // tile) * tile, tile), tile)
        f = fc[:, i, where].reshape(ins, width)
        f_high = f.astype(jnp.bfloat16)
        f_low = (f - f_high.astype(jnp.float32)).astype(jnp.bfloat16)
        value = dot16(wide_high, f_high) + (dot16(wide_high, f_low) + dot16(wide_low, f_high))
        out[:, i, where] = value.reshape(members, tile, width)

    @pl.when(has_high)
    def _():
        chalo_up().wait_send()
        chalo_pass(1).wait_send()

    @pl.when(has_low)
    def _():
        chalo_down().wait_send()
        chalo_pass(0).wait_send()

    @pl.loop(0, members)
    def _(m):
        @pl.when(has_high)
        def _():
            halo_up(m).wait_send()

        @pl.when(has_low)
        def _():
            halo_down(m).wait_send()

        for d in range(1, chips):
            send_x(d, m).wait_send()
        for d in range(chips):
            send_p(d, m).wait_send()

    for d in range(1, mem_n):
        remote(prof.at[mine], prof.at[mine], q_send.at[d], q_recv.at[mem], row, lax.rem(mem + d, mem_n)).wait_send()
    for d in range(1, rows_n):
        remote(grec.at[row], grec.at[row], g_send.at[d], g_recv.at[row], lax.rem(row + d, rows_n), mem).wait_send()


def per_device(rows_n, mem_n, ensemble, courant, obs_column, obs_value, obs_var):
    members, levels, rows, width = ensemble.shape
    nobs = obs_column.shape[0]
    chips = mem_n // 2
    local = obs_column - lax.axis_index("rows") * (rows * width)
    f32 = jnp.float32
    vmem = pl.BlockSpec(memory_space=pltpu.VMEM)
    smem = pl.BlockSpec(memory_space=pltpu.SMEM)
    dma = pltpu.SemaphoreType.DMA
    total = members * mem_n
    plane = (levels, width)
    result = pl.pallas_call(
        functools.partial(kernel, rows_n, mem_n),
        out_shape=jax.ShapeDtypeStruct((members, rows, levels, width), f32),
        in_specs=[vmem, vmem, smem, smem, vmem, vmem],
        out_specs=vmem,
        scratch_shapes=[
            pltpu.VMEM((2, 2, 3) + plane, f32),
            pltpu.VMEM((members, 2, 3) + plane, f32),
            pltpu.VMEM((rows + 4, 7) + plane, f32),
            pltpu.VMEM((rows + 6,) + plane, f32),
            pltpu.VMEM((rows + 4,) + plane, f32),
            pltpu.VMEM((rows + 2,) + plane, f32),
            pltpu.VMEM((rows,) + plane, f32),
            pltpu.VMEM((total, rows) + plane, f32),
            pltpu.VMEM((nobs * levels, LANES), f32),
            pltpu.VMEM((total, nobs * levels), f32),
            pltpu.VMEM((rows_n, total, LANES), f32),
            pltpu.VMEM((total, total), f32),
            dma((2,)), dma((2,)), dma((2,)), dma((2,)),
            dma((2, members)), dma((2, members)),
            dma((chips, members)), dma((chips, members)), dma((mem_n, members)),
            dma((mem_n,)), dma((mem_n,)),
            dma((rows_n,)), dma((rows_n,)),
        ],
        compiler_params=pltpu.CompilerParams(
            collective_id=0, has_side_effects=True, vmem_limit_bytes=60 * 1024 * 1024
        ),
    )(
        ensemble.transpose(0, 2, 1, 3),
        courant.transpose(0, 2, 1, 3),
        local // width,
        local % width,
        obs_value.T,
        obs_var.T,
    )
    return result.transpose(0, 2, 1, 3)


def solution(mesh):
    return jax.shard_map(
        functools.partial(per_device, mesh.shape["rows"], mesh.shape["mem"]),
        mesh=mesh,
        in_specs=(
            P("mem", None, "rows", None),
            P(None, None, "rows", None),
            P("rows"),
            P(None, "rows"),
            P(None, "rows"),
        ),
        out_specs=P("mem", None, "rows", None),
        check_vma=False,
    )
```

profile of v0, /device:TPU:25, one launch (start us, length us, event | category | flops | bytes accessed | tf_op | source)
XLA Modules:
  0.0 163.5 jit_solution(7812569074525189902)
XLA Ops:
  0.0 1.2 and_select_fusion
  1.2 157.3 %shard_map.55 = f32[16,6,32,384]{3,2,1,0:T(8,128)} custom-call(f32[16,6,32,384]{3,2,1,0:T(8,128)} %bitcast.6, f32[3,6,32,384]{3,2,1,0:T(8,128)} %bitcast.7, s32[16]{0:T(128)} %get-tuple-element.6.obs_x, s32[16]{0:T(128)} %get-tuple-element.5.obs_y, f32[16,32]{1,0:T(8,128)} %bitcast.8, f32[16,32]{1,0:T(8,128)} %bitcast.9), custom_call_target="tpu_custom_call" | custom-call | tf_op jit(solution)/shard_map/pallas_call | solution.py:363
  158.5 5.0 %copy.7 = f32[16,32,6,384]{3,1,2,0:T(8,128)} copy(f32[16,32,6,384]{3,1,2,0:T(8,128)} %bitcast.5) | data formatting | bytes 9437184
where the time goes:
time: 166 us; the launch traced here: 164 us
  Pallas kernels  157 us (95%)
  local copies, waits for them, and re-layouts  5.01 us (3%)
    pallas_call x1, Pallas kernels, per_device(): pl.pallas_call(functools.partial(kernel, rows_n, mem_n), out_shape=jax.Sh...  157 us
    unnamed x1, local copies, waits for them, and re-layouts  5.01 us

commit v1 on v0

v1 whole, which is shorter than its diff:
```python
import functools

import jax
import jax.numpy as jnp
from jax import lax
from jax.experimental import pallas as pl
from jax.experimental.pallas import tpu as pltpu
from jax.sharding import PartitionSpec as P

NS_ITERS = 4
DIFFUSION = 0.05
AHEAD = 2
LAG = 2
LANES = 128
TILE = 8
MESH = pl.DeviceIdType.MESH
HIGHEST = lax.Precision.HIGHEST


def cdiv(a, b):
    return -(-a // b)


def kernel(
    rows_n, mem_n,
    ens_any, cour_any, obs, obs_value, obs_var,
    out,
    ens, cour, chalo, chalo3, hal, coef, cext, w0, w1, w2, z0, z1, z2, z3, fc,
    obsv, hot, pp, prec, prof, scal, grec, gall, wts, wsp,
    e_load, c_load,
    c_send, c_recv, cf_send, cf_recv, d_send, d_recv, df_send, df_recv, o_send, o_recv,
    h_send, h_recv,
    x_send, p_send, f_recv, r_send, r_recv, q_send, q_recv, g_send, g_recv, a_send, a_recv,
):
    members, rows, levels, width = ens.shape
    total = members * mem_n
    nobs = obs.shape[0]
    chips = mem_n // 2
    groups = levels // TILE
    row = lax.axis_index("rows")
    mem = lax.axis_index("mem")
    core = lax.rem(mem, 2)
    chip = mem // 2
    partner = chip * 2 + 1 - core
    f32 = jnp.float32

    def remote(src, dst, ssem, rsem, r, m):
        return pltpu.make_async_remote_copy(
            src_ref=src, dst_ref=dst, send_sem=ssem, recv_sem=rsem,
            device_id=(r, m), device_id_type=MESH,
        )

    def load_cour():
        return pltpu.make_async_copy(cour_any, cour, c_load.at[0])

    def load_ens(m):
        return pltpu.make_async_copy(ens_any.at[m], ens.at[m], e_load.at[m])

    load_cour().start()

    @pl.loop(0, members)
    def _(m):
        load_ens(m).start()

    barrier = pltpu.get_barrier_semaphore()
    for d in range(1, mem_n):
        pl.semaphore_signal(barrier, inc=1, device_id=(row, lax.rem(mem + d, mem_n)), device_id_type=MESH)
    for d in range(1, rows_n):
        pl.semaphore_signal(barrier, inc=1, device_id=(lax.rem(row + d, rows_n), mem), device_id_type=MESH)

    has_low = row > 0
    has_high = row < rows_n - 1
    low = jnp.maximum(row - 1, 0)
    high = jnp.minimum(row + 1, rows_n - 1)

    lane = lax.broadcasted_iota(jnp.int32, (TILE, LANES), 1)
    slot = lax.rem(lane, nobs)
    ox = jnp.zeros((TILE, LANES), jnp.int32)
    oy = jnp.zeros((TILE, LANES), jnp.int32)
    for p in range(nobs):
        gx = lax.div(obs[p], width)
        ox = jnp.where(slot == p, gx, ox)
        oy = jnp.where(slot == p, obs[p] - gx * width, oy)
    obsv[0, 0] = ox
    obsv[0, 1] = oy

    load_cour().wait()
    load_ens(0).wait()
    pl.semaphore_wait(barrier, mem_n - 1 + rows_n - 1)

    def chalo_up():
        return remote(cour.at[:, rows - 2 + core], chalo.at[0, core], c_send.at[0], c_recv.at[0], high, mem)

    def chalo_down():
        return remote(cour.at[:, core], chalo.at[1, core], c_send.at[1], c_recv.at[1], low, mem)

    def chalo_pass(side):
        return remote(chalo.at[side, core], chalo.at[side, core], cf_send.at[side], cf_recv.at[side], row, partner)

    def far_up():
        return remote(cour.at[0, rows - 3], chalo3.at[0], d_send.at[0], d_recv.at[0], high, mem)

    def far_down():
        return remote(cour.at[0, 2], chalo3.at[1], d_send.at[1], d_recv.at[1], low, mem)

    def far_pass(side):
        return remote(chalo3.at[side], chalo3.at[side], df_send.at[side], df_recv.at[side], row, partner)

    def obs_up():
        return remote(obsv.at[0], obsv.at[1], o_send.at[0], o_recv.at[0], high, mem)

    def obs_down():
        return remote(obsv.at[0], obsv.at[2], o_send.at[1], o_recv.at[1], low, mem)

    def halo_up(m):
        return remote(ens.at[m, pl.ds(rows - 3, 3)], hal.at[m, 0], h_send.at[0, m], h_recv.at[0, m], high, mem)

    def halo_down(m):
        return remote(ens.at[m, pl.ds(0, 3)], hal.at[m, 1], h_send.at[1, m], h_recv.at[1, m], low, mem)

    first = core == 0

    @pl.when(has_high)
    def _():
        chalo_up().start()

    @pl.when(has_low)
    def _():
        chalo_down().start()

    def send_halo(m):
        @pl.when(has_high)
        def _():
            halo_up(m).start()

        @pl.when(has_low)
        def _():
            halo_down(m).start()

    send_halo(0)

    @pl.when(has_high)
    def _():
        obs_up().start()

        @pl.when(first)
        def _():
            far_up().start()

    @pl.when(has_low)
    def _():
        obs_down().start()

        @pl.when(first)
        def _():
            far_down().start()

    ahead = min(AHEAD, members)

    @pl.loop(1, members)
    def _(m):
        load_ens(m).wait()

    @pl.loop(1, ahead)
    def _(m):
        send_halo(m)

    level = lax.broadcasted_iota(jnp.int32, (levels, width), 0)
    cell = lax.broadcasted_iota(jnp.int32, (levels, width), 1)

    def set_coef(i, a0, a1, a2):
        coef[i, 0] = 1.0 - 6.0 * DIFFUSION - jnp.abs(a0) - jnp.abs(a1) - jnp.abs(a2)
        coef[i, 1] = DIFFUSION + jnp.maximum(a0, 0.0)
        coef[i, 2] = DIFFUSION - jnp.minimum(a0, 0.0)
        coef[i, 3] = jnp.where(cell > 0, DIFFUSION + jnp.maximum(a1, 0.0), 0.0)
        coef[i, 4] = jnp.where(cell < width - 1, DIFFUSION - jnp.minimum(a1, 0.0), 0.0)
        coef[i, 5] = jnp.where(level > 0, DIFFUSION + jnp.maximum(a2, 0.0), 0.0)
        coef[i, 6] = jnp.where(level < levels - 1, DIFFUSION - jnp.minimum(a2, 0.0), 0.0)

    @pl.loop(0, rows)
    def _(i):
        set_coef(i + 2, cour[0, i], cour[1, i], cour[2, i])

    def clear(ref, start, count):
        ref[pl.ds(start, count)] = jnp.zeros((count, levels, width), f32)

    @pl.loop(0, members)
    def _(m):
        out[m] = jnp.zeros((rows, levels, width), f32)

    clear(z0, 0, 1)
    clear(z0, rows + 1, 1)
    clear(z1, 0, 1)
    clear(z1, rows + 3, 1)
    clear(z2, 0, 1)
    clear(z2, rows + 5, 1)

    @pl.when(jnp.logical_not(has_low))
    def _():
        clear(w0, 0, 3)
        coef[pl.ds(0, 2)] = jnp.zeros((2, 7, levels, width), f32)
        cext[0] = jnp.zeros((levels, width), f32)
        obsv[1] = jnp.full((2, TILE, LANES), -1, jnp.int32)
        prec[0] = jnp.zeros((groups, members, LANES), f32)

    @pl.when(jnp.logical_not(has_high))
    def _():
        clear(w0, rows + 3, 3)
        coef[pl.ds(rows + 2, 2)] = jnp.zeros((2, 7, levels, width), f32)
        cext[1] = jnp.zeros((levels, width), f32)
        obsv[2] = jnp.full((2, TILE, LANES), -1, jnp.int32)
        prec[1] = jnp.zeros((groups, members, LANES), f32)

    def edge(side, present, begin):
        @pl.when(present)
        def _():
            (chalo_down if side else chalo_up)().wait_recv()
            chalo_pass(side).start()
            (obs_down if side else obs_up)().wait_recv()

            @pl.when(first)
            def _():
                (far_down if side else far_up)().wait_recv()
                far_pass(side).start()

            @pl.when(jnp.logical_not(first))
            def _():
                far_pass(side).wait_recv()

            chalo_pass(side).wait_recv()

            @pl.loop(0, 2)
            def _(i):
                set_coef(begin + i, chalo[side, i, 0], chalo[side, i, 1], chalo[side, i, 2])

            a0 = chalo3[side]
            cext[side] = DIFFUSION + (jnp.maximum(a0, 0.0) if side else -jnp.minimum(a0, 0.0))

    edge(0, has_low, 0)
    edge(1, has_high, rows + 2)

    for k in range(3):
        hot[k] = jnp.where(
            lax.broadcasted_iota(jnp.int32, (width, LANES), 0) == obsv[k, 1, :1], 1.0, 0.0
        ).astype(jnp.bfloat16)

    def update(src, i, c):
        mid = src[i + 1]
        return (
            coef[c, 0] * mid
            + coef[c, 1] * src[i]
            + coef[c, 2] * src[i + 2]
            + coef[c, 3] * pltpu.roll(mid, 1, 1)
            + coef[c, 4] * pltpu.roll(mid, width - 1, 1)
            + coef[c, 5] * pltpu.roll(mid, 1, 0)
            + coef[c, 6] * pltpu.roll(mid, levels - 1, 0)
        )

    def other(d):
        return lax.rem(chip + d, chips) * 2 + core

    def send_x(d, m):
        slot = fc.at[mem * members + m]
        return remote(slot, slot, x_send.at[d, m], f_recv.at[mem, m], row, other(d))

    def send_p(d, m):
        src = lax.rem(chip + d, chips) * 2 + core
        slot = fc.at[src * members + m]
        return remote(slot, slot, p_send.at[d, m], f_recv.at[src, m], row, partner)

    def arrived(src, m):
        slot = fc.at[src * members + m]
        return remote(slot, slot, p_send.at[0, 0], f_recv.at[src, m], row, partner)

    def forward(m):
        for d in range(1, chips):
            arrived(other(d), m).wait_recv()
            send_p(d, m).start()

    def service(m):
        @pl.when(has_low)
        def _():
            halo_up(m).wait_recv()
            w0[pl.ds(0, 3)] = hal[m, 0]

        @pl.when(has_high)
        def _():
            halo_down(m).wait_recv()
            w0[pl.ds(rows + 3, 3)] = hal[m, 1]

        @pl.when(m + ahead < members)
        def _():
            send_halo(m + ahead)

        w0[pl.ds(3, rows)] = ens[m]

        @pl.loop(0, rows + 4, unroll=2)
        def _(i):
            w1[i] = update(w0, i, i)

        @pl.loop(0, rows + 2, unroll=2)
        def _(i):
            w2[i] = update(w1, i, i + 1)

        @pl.loop(0, rows, unroll=2)
        def _(i):
            fc[mem * members + m, i] = update(w2, i, i + 2)

        for d in range(1, chips):
            send_x(d, m).start()
        send_p(0, m).start()

        @pl.when(m >= LAG)
        def _():
            forward(m - LAG)

    inside = lax.broadcasted_iota(jnp.int32, (levels, LANES), 0)
    owner = lax.broadcasted_iota(jnp.int32, (levels, LANES), 1) // nobs
    pick = lax.rem(inside, TILE) == owner

    def fold(x):
        return jnp.sum(jnp.where(pick, x, 0.0).reshape(groups, TILE, LANES), axis=1)

    def profile(m):
        z0[pl.ds(1, rows)] = ens[m]
        z1[1] = coef[1, 2] * z0[1]
        z1[rows + 2] = coef[rows + 2, 1] * z0[rows]

        @pl.loop(0, rows, unroll=2)
        def _(i):
            z1[i + 2] = update(z0, i, i + 2)

        z2[1] = coef[0, 2] * z1[1]
        z2[rows + 4] = coef[rows + 3, 1] * z1[rows + 2]

        @pl.loop(0, rows + 2, unroll=2)
        def _(i):
            z2[i + 2] = update(z1, i, i + 1)

        z3[0] = cext[0] * z2[1]
        z3[rows + 5] = cext[1] * z2[rows + 4]

        @pl.loop(0, rows + 4, unroll=2)
        def _(i):
            z3[i + 1] = update(z2, i, i)

        for k, begin, count in ((0, 3, rows), (1, 0, 3), (2, rows + 3, 3)):
            x = z3[pl.ds(begin, count)].reshape(count * levels, width)
            high_part = x.astype(jnp.bfloat16)
            low_part = (x - high_part.astype(f32)).astype(jnp.bfloat16)
            got = jnp.dot(high_part, hot[k], preferred_element_type=f32)
            got = got + jnp.dot(low_part, hot[k], preferred_element_type=f32)
            at = obsv[k, 0, :1] - row * rows + 3
            acc = jnp.zeros((levels, LANES), f32)
            for i in range(count):
                acc = acc + jnp.where(at == begin + i, got[i * levels:(i + 1) * levels], 0.0)
            pp[k, :, pl.ds(m, 1)] = fold(acc)[:, None]

    def dot(a, b):
        return jnp.dot(a, b, precision=HIGHEST, preferred_element_type=f32)

    mine = pl.ds(pl.multiple_of(mem * members, members), members)

    def give_low():
        return remote(pp.at[1], prec.at[1], r_send.at[1], r_recv.at[1], low, mem)

    def give_high():
        return remote(pp.at[2], prec.at[0], r_send.at[0], r_recv.at[0], high, mem)

    def stage_a():
        @pl.when(has_high)
        def _():
            give_high().start()

        @pl.when(has_low)
        def _():
            give_low().start()

    def give_prof(d):
        block = prof.at[:, mine]
        return remote(block, block, q_send.at[d], q_recv.at[mem], row, lax.rem(mem + d, mem_n))

    def stage_b():
        @pl.when(has_low)
        def _():
            give_high().wait_recv()

        @pl.when(has_high)
        def _():
            give_low().wait_recv()

        prof[:, mine] = pp[0] + prec[0] + prec[1]
        for d in range(1, mem_n):
            give_prof(d).start()

    def flat(ref):
        repeat = lax.broadcasted_iota(jnp.int32, (nobs, LANES), 1) % nobs
        repeat = jnp.where(repeat == lax.broadcasted_iota(jnp.int32, (nobs, LANES), 0), 1.0, 0.0).astype(f32)
        got = fold(dot(ref[...].T, repeat))
        return jnp.concatenate([got[q:q + 1] for q in range(groups)], axis=1)

    def give_gram(d):
        return remote(grec.at[row], grec.at[row], g_send.at[d], g_recv.at[row], lax.rem(row + d, rows_n), mem)

    def stage_c():
        for d in range(1, mem_n):
            src = lax.rem(mem + d, mem_n)
            block = prof.at[:, pl.ds(pl.multiple_of(src * members, members), members)]
            remote(block, block, q_send.at[d], q_recv.at[src], row, src).wait_recv()
        values = jnp.concatenate([prof[q] for q in range(groups)], axis=1)
        variance = flat(obs_var)
        center = jnp.mean(values, axis=0, keepdims=True)
        scaled = (values - center) / jnp.sqrt((total - 1.0) * variance)
        innovation = (flat(obs_value) - center) / jnp.sqrt(variance)
        pad = jnp.broadcast_to(innovation, (LANES - total, innovation.shape[1]))
        scal[...] = scaled
        both = jnp.concatenate([scaled, pad], axis=0)
        grec[row] = lax.dot_general(
            scal[mine], both, (((1,), (1,)), ((), ())), precision=HIGHEST, preferred_element_type=f32
        )
        for d in range(1, rows_n):
            give_gram(d).start()

    def give_sum(d):
        return remote(gall.at[mine], gall.at[mine], a_send.at[d], a_recv.at[mem], row, lax.rem(mem + d, mem_n))

    def stage_d():
        for d in range(1, rows_n):
            src = lax.rem(row + d, rows_n)
            remote(grec.at[src], grec.at[src], g_send.at[d], g_recv.at[src], src, mem).wait_recv()
        part = grec[0]
        for r in range(1, rows_n):
            part = part + grec[r]
        gall[mine] = part
        for d in range(1, mem_n):
            give_sum(d).start()

    def stage_e():
        for d in range(1, mem_n):
            src = lax.rem(mem + d, mem_n)
            block = gall.at[pl.ds(pl.multiple_of(src * members, members), members)]
            remote(block, block, a_send.at[d], a_recv.at[src], row, src).wait_recv()
        gsum = gall[...]
        ri = lax.broadcasted_iota(jnp.int32, (total, total), 0)
        ci = lax.broadcasted_iota(jnp.int32, (total, total), 1)
        eye = jnp.where(ri == ci, 1.0, 0.0).astype(f32)
        system = eye + gsum[:, :total]
        frob = jnp.sqrt(jnp.sum(jnp.sum(system * system, axis=1, keepdims=True), axis=0, keepdims=True))
        y = system / frob
        z = eye
        for it in range(NS_ITERS):
            factor = 0.5 * (3.0 * eye - (y if it == 0 else dot(z, y)))
            if it < NS_ITERS - 1:
                y = dot(y, factor)
            z = factor if it == 0 else dot(factor, z)
        root = z / jnp.sqrt(frob)
        shift = dot(root, dot(root, gsum))[:, total:total + 1] / jnp.sqrt(f32(total - 1.0))
        mixed = shift + root
        weights = 1.0 / total + mixed - jnp.mean(mixed, axis=0, keepdims=True)
        wts[...] = weights.T
        own = wts[mine].T
        for k in range(members):
            wsp[k] = jnp.broadcast_to(own[:, k:k + 1], (total, LANES))

    block = min(4, members)
    tiles = width // LANES

    def mix(m):
        for d in range(chips):
            arrived(lax.rem(chip + d, chips) * 2 + 1 - core, m).wait_recv()

        @pl.loop(0, members // block)
        def _(b):
            ws = [
                [
                    jnp.broadcast_to(wsp[b * block + k, pl.ds(s * members + m, 1)], (TILE, LANES))
                    for s in range(mem_n)
                ]
                for k in range(block)
            ]

            @pl.loop(0, rows)
            def _(i):
                for t in range(groups):
                    for c in range(tiles):
                        at = (i, pl.ds(t * TILE, TILE), pl.ds(c * LANES, LANES))
                        f = [fc[(s * members + m,) + at] for s in range(mem_n)]
                        for k in range(block):
                            acc = out[(b * block + k,) + at]
                            for s in range(mem_n):
                                acc = acc + ws[k][s] * f[s]
                            out[(b * block + k,) + at] = acc

    passes = min(4, members)
    per_pass = cdiv(members, passes)
    gap = max(1, (members - passes) // 6)
    at_a = passes - 1
    at_b, at_c, at_d, at_e = (at_a + gap * n for n in range(1, 5))
    per_mix = 3
    mixed_in_loop = max(0, members - 1 - at_e) * per_mix
    assert at_e < members and mixed_in_loop <= members - LAG

    @pl.loop(0, members)
    def _(m):
        service(m)

        @pl.when(m < passes)
        def _():
            @pl.loop(0, per_pass)
            def _(n):
                profile(m * per_pass + n)

        for at, stage in ((at_a, stage_a), (at_b, stage_b), (at_c, stage_c), (at_d, stage_d), (at_e, stage_e)):
            pl.when(m == at)(stage)

        @pl.when(m > at_e)
        def _():
            @pl.loop(0, per_mix)
            def _(n):
                mix((m - at_e - 1) * per_mix + n)

    @pl.loop(members - LAG, members)
    def _(m):
        forward(m)

    @pl.loop(mixed_in_loop, members)
    def _(m):
        mix(m)

    @pl.when(has_high)
    def _():
        chalo_up().wait_send()
        chalo_pass(1).wait_send()
        obs_up().wait_send()
        give_high().wait_send()

        @pl.when(first)
        def _():
            far_up().wait_send()
            far_pass(1).wait_send()

    @pl.when(has_low)
    def _():
        chalo_down().wait_send()
        chalo_pass(0).wait_send()
        obs_down().wait_send()
        give_low().wait_send()

        @pl.when(first)
        def _():
            far_down().wait_send()
            far_pass(0).wait_send()

    @pl.loop(0, members)
    def _(m):
        @pl.when(has_high)
        def _():
            halo_up(m).wait_send()

        @pl.when(has_low)
        def _():
            halo_down(m).wait_send()

        for d in range(1, chips):
            send_x(d, m).wait_send()
        for d in range(chips):
            send_p(d, m).wait_send()

    for d in range(1, mem_n):
        give_prof(d).wait_send()
        give_sum(d).wait_send()
    for d in range(1, rows_n):
        give_gram(d).wait_send()


def per_device(rows_n, mem_n, ensemble, courant, obs_column, obs_value, obs_var):
    members, levels, rows, width = ensemble.shape
    nobs = obs_column.shape[0]
    chips = mem_n // 2
    groups = levels // TILE
    f32 = jnp.float32
    vmem = pl.BlockSpec(memory_space=pltpu.VMEM)
    smem = pl.BlockSpec(memory_space=pltpu.SMEM)
    hbm = pl.BlockSpec(memory_space=pl.ANY)
    dma = pltpu.SemaphoreType.DMA
    total = members * mem_n
    plane = (levels, width)
    result = pl.pallas_call(
        functools.partial(kernel, rows_n, mem_n),
        out_shape=pltpu.VMEM((members, rows) + plane, f32),
        in_specs=[hbm, hbm, smem, vmem, vmem],
        out_specs=vmem,
        scratch_shapes=[
            pltpu.VMEM((members, rows) + plane, f32),
            pltpu.VMEM((3, rows) + plane, f32),
            pltpu.VMEM((2, 2, 3) + plane, f32),
            pltpu.VMEM((2,) + plane, f32),
            pltpu.VMEM((members, 2, 3) + plane, f32),
            pltpu.VMEM((rows + 4, 7) + plane, f32),
            pltpu.VMEM((2,) + plane, f32),
            pltpu.VMEM((rows + 6,) + plane, f32),
            pltpu.VMEM((rows + 4,) + plane, f32),
            pltpu.VMEM((rows + 2,) + plane, f32),
            pltpu.VMEM((rows + 2,) + plane, f32),
            pltpu.VMEM((rows + 4,) + plane, f32),
            pltpu.VMEM((rows + 6,) + plane, f32),
            pltpu.VMEM((rows + 6,) + plane, f32),
            pltpu.VMEM((total, rows) + plane, f32),
            pltpu.VMEM((3, 2, TILE, LANES), jnp.int32),
            pltpu.VMEM((3, width, LANES), jnp.bfloat16),
            pltpu.VMEM((3, groups, members, LANES), f32),
            pltpu.VMEM((2, groups, members, LANES), f32),
            pltpu.VMEM((groups, total, LANES), f32),
            pltpu.VMEM((total, groups * LANES), f32),
            pltpu.VMEM((rows_n, members, LANES), f32),
            pltpu.VMEM((total, LANES), f32),
            pltpu.VMEM((total, total), f32),
            pltpu.VMEM((members, total, LANES), f32),
            dma((members,)), dma((1,)),
            dma((2,)), dma((2,)), dma((2,)), dma((2,)),
            dma((2,)), dma((2,)), dma((2,)), dma((2,)), dma((2,)), dma((2,)),
            dma((2, members)), dma((2, members)),
            dma((chips, members)), dma((chips, members)), dma((mem_n, members)),
            dma((2,)), dma((2,)),
            dma((mem_n,)), dma((mem_n,)),
            dma((rows_n,)), dma((rows_n,)),
            dma((mem_n,)), dma((mem_n,)),
        ],
        compiler_params=pltpu.CompilerParams(
            collective_id=0, has_side_effects=True, vmem_limit_bytes=52 * 1024 * 1024
        ),
    )(
        ensemble.transpose(0, 2, 1, 3),
        courant.transpose(0, 2, 1, 3),
        obs_column,
        obs_value.T,
        obs_var.T,
    )
    return result.transpose(0, 2, 1, 3)


def solution(mesh):
    return jax.shard_map(
        functools.partial(per_device, mesh.shape["rows"], mesh.shape["mem"]),
        mesh=mesh,
        in_specs=(
            P("mem", None, "rows", None),
            P(None, None, "rows", None),
            P("rows"),
            P(None, "rows"),
            P(None, "rows"),
        ),
        out_specs=P("mem", None, "rows", None),
        check_vma=False,
    )
```

time: 166 us -> 159 us (0.958)
  the two profiles are of different devices: /device:TPU:25 before, /device:TPU:8 now
where the time goes in v1:
time: 159 us; the launch traced here: 158 us
  Pallas kernels  156 us (98%)
  local copies, waits for them, and re-layouts  2.19 us (1%)
    pallas_call x1, Pallas kernels, per_device(): pl.pallas_call(functools.partial(kernel, rows_n, mem_n), out_shape=pltpu....  156 us

profile of v1, /device:TPU:8, one launch (start us, length us, event | category | flops | bytes accessed | tf_op | source)
XLA Modules:
  0.0 158.4 jit_solution(1705994961295864134)
XLA Ops:
  0.0 156.2 %shard_map.55 = f32[16,6,32,384]{3,2,1,0:T(8,128)S(1)} custom-call(f32[16,6,32,384]{3,2,1,0:T(8,128)} %bitcast.6, f32[3,6,32,384]{3,2,1,0:T(8,128)} %bitcast.7, s32[16]{0:T(128)} %obs.1, f32[16,32]{1,0:T(8,128)} %bitcast.8, f32[16,32]{1,0:T(8,128)} %bitcast.9), custom_call_target="tpu_custom_call" | custom-call | tf_op jit(solution)/shard_map/pallas_call | solution.py:588
  156.2 2.2 %copy.7 = f32[16,32,6,384]{3,1,2,0:T(8,128)} copy(f32[16,32,6,384]{3,1,2,0:T(8,128)S(1)} %bitcast.5) | data formatting | bytes 9437184

commit v2 on v1

--- a/solution.py
+++ b/solution.py
@@ -9,27 +9,29 @@
 
 NS_ITERS = 4
 DIFFUSION = 0.05
-AHEAD = 2
+NEAR = 2
+FAR = 1
+DETOUR = 3
+RELAY = 1
 LAG = 2
+PER_PASS = 4
+STAGES = (2, 4, 6, 6)
+PER_MIX = 3
 LANES = 128
 TILE = 8
 MESH = pl.DeviceIdType.MESH
 HIGHEST = lax.Precision.HIGHEST
 
 
-def cdiv(a, b):
-    return -(-a // b)
-
-
 def kernel(
     rows_n, mem_n,
     ens_any, cour_any, obs, obs_value, obs_var,
     out,
-    ens, cour, chalo, chalo3, hal, coef, cext, w0, w1, w2, z0, z1, z2, z3, fc,
+    ens, cour, chalo, chalo3, hal, coef, cext, w1, w2, z1, z2, zb, rbuf, fc,
     obsv, hot, pp, prec, prof, scal, grec, gall, wts, wsp,
     e_load, c_load,
     c_send, c_recv, cf_send, cf_recv, d_send, d_recv, df_send, df_recv, o_send, o_recv,
-    h_send, h_recv,
+    h_send, h_recv, rb_recv, rf_send,
     x_send, p_send, f_recv, r_send, r_recv, q_send, q_recv, g_send, g_recv, a_send, a_recv,
 ):
     members, rows, levels, width = ens.shape
@@ -120,50 +122,94 @@
 
     first = core == 0
 
+    odd = lax.rem(row, 2) == 1
+    ahead_up = jnp.where(odd, FAR, NEAR)
+    ahead_down = jnp.where(odd, NEAR, FAR)
+
+    pairs = max(1, rows_n // 2)
+    pair = row // 2
+    send_limit = jnp.where(odd, pair, pairs - 1 - pair)
+    relay_limit = jnp.where(odd, pairs - 1 - pair, pair)
+    relay_side = jnp.where(odd, 1, 0)
+    relay_on = jnp.logical_and(jnp.where(odd, row - 2, row) >= 0, jnp.where(odd, row, row + 2) < rows_n)
+    relay_row = jnp.clip(jnp.where(odd, row - 2, row + 2), 0, rows_n - 1)
+
+    def detour(m):
+        return jnp.logical_and(lax.rem(m, pairs) > send_limit, jnp.logical_and(has_low, has_high))
+
+    def send_up(m):
+        @pl.when(jnp.logical_and(has_high, jnp.logical_not(jnp.logical_and(odd, detour(m)))))
+        def _():
+            halo_up(m).start()
+
+    def send_down(m):
+        @pl.when(jnp.logical_and(has_low, jnp.logical_or(odd, jnp.logical_not(detour(m)))))
+        def _():
+            halo_down(m).start()
+
+    def send_detour(m):
+        @pl.when(jnp.logical_and(odd, detour(m)))
+        def _():
+            remote(ens.at[m, pl.ds(rows - 3, 3)], rbuf.at[m], h_send.at[0, m], rb_recv.at[m], low, mem).start()
+
+        @pl.when(jnp.logical_and(jnp.logical_not(odd), detour(m)))
+        def _():
+            remote(ens.at[m, pl.ds(0, 3)], rbuf.at[m], h_send.at[1, m], rb_recv.at[m], high, mem).start()
+
+    def relays(m):
+        return jnp.logical_and(lax.rem(m, pairs) > relay_limit, relay_on)
+
+    def relay_out(m):
+        return remote(
+            rbuf.at[m], hal.at[m, relay_side], rf_send.at[m], h_recv.at[relay_side, m], relay_row, mem
+        )
+
+    def relay(m):
+        @pl.when(relays(m))
+        def _():
+            remote(rbuf.at[m], rbuf.at[m], rf_send.at[m], rb_recv.at[m], high, mem).wait_recv()
+            relay_out(m).start()
+
     @pl.when(has_high)
     def _():
         chalo_up().start()
 
+        @pl.when(first)
+        def _():
+            far_up().start()
+
+        obs_up().start()
+
     @pl.when(has_low)
     def _():
         chalo_down().start()
 
-    def send_halo(m):
-        @pl.when(has_high)
-        def _():
-            halo_up(m).start()
-
-        @pl.when(has_low)
-        def _():
-            halo_down(m).start()
-
-    send_halo(0)
-
-    @pl.when(has_high)
-    def _():
-        obs_up().start()
-
         @pl.when(first)
         def _():
-            far_up().start()
-
-    @pl.when(has_low)
-    def _():
+            far_down().start()
+
         obs_down().start()
-
-        @pl.when(first)
-        def _():
-            far_down().start()
-
-    ahead = min(AHEAD, members)
 
     @pl.loop(1, members)
     def _(m):
         load_ens(m).wait()
 
-    @pl.loop(1, ahead)
-    def _(m):
-        send_halo(m)
+    def start_halos(near):
+        @pl.when(odd == near)
+        def _():
+            @pl.loop(0, ahead_down)
+            def _(m):
+                send_down(m)
+
+        @pl.when(odd != near)
+        def _():
+            @pl.loop(0, ahead_up)
+            def _(m):
+                send_up(m)
+
+    start_halos(True)
+    for m in range(FAR, DETOUR):
+        send_detour(m)
 
     level = lax.broadcasted_iota(jnp.int32, (levels, width), 0)
     cell = lax.broadcasted_iota(jnp.int32, (levels, width), 1)
@@ -181,23 +227,18 @@
     def _(i):
         set_coef(i + 2, cour[0, i], cour[1, i], cour[2, i])
 
-    def clear(ref, start, count):
-        ref[pl.ds(start, count)] = jnp.zeros((count, levels, width), f32)
-
     @pl.loop(0, members)
     def _(m):
         out[m] = jnp.zeros((rows, levels, width), f32)
 
-    clear(z0, 0, 1)
-    clear(z0, rows + 1, 1)
-    clear(z1, 0, 1)
-    clear(z1, rows + 3, 1)
-    clear(z2, 0, 1)
-    clear(z2, rows + 5, 1)
+    def no_halo(side):
+        @pl.loop(0, members)
+        def _(m):
+            hal[m, side] = jnp.zeros((3, levels, width), f32)
 
     @pl.when(jnp.logical_not(has_low))
     def _():
-        clear(w0, 0, 3)
+        no_halo(0)
         coef[pl.ds(0, 2)] = jnp.zeros((2, 7, levels, width), f32)
         cext[0] = jnp.zeros((levels, width), f32)
         obsv[1] = jnp.full((2, TILE, LANES), -1, jnp.int32)
@@ -205,7 +246,7 @@
 
     @pl.when(jnp.logical_not(has_high))
     def _():
-        clear(w0, rows + 3, 3)
+        no_halo(1)
         coef[pl.ds(rows + 2, 2)] = jnp.zeros((2, 7, levels, width), f32)
         cext[1] = jnp.zeros((levels, width), f32)
         obsv[2] = jnp.full((2, TILE, LANES), -1, jnp.int32)
@@ -236,20 +277,38 @@
             a0 = chalo3[side]
             cext[side] = DIFFUSION + (jnp.maximum(a0, 0.0) if side else -jnp.minimum(a0, 0.0))
 
-    edge(0, has_low, 0)
-    edge(1, has_high, rows + 2)
-
-    for k in range(3):
-        hot[k] = jnp.where(
-            lax.broadcasted_iota(jnp.int32, (width, LANES), 0) == obsv[k, 1, :1], 1.0, 0.0
-        ).astype(jnp.bfloat16)
-
-    def update(src, i, c):
-        mid = src[i + 1]
+    @pl.when(odd)
+    def _():
+        edge(0, has_low, 0)
+
+    @pl.when(jnp.logical_not(odd))
+    def _():
+        edge(1, has_high, rows + 2)
+
+    start_halos(False)
+
+    @pl.when(odd)
+    def _():
+        edge(1, has_high, rows + 2)
+
+    @pl.when(jnp.logical_not(odd))
+    def _():
+        edge(0, has_low, 0)
+
+    def set_hot(k):
+        hit = lax.broadcasted_iota(jnp.int32, (width, LANES), 0) == obsv[k, 1, :1]
+        hit = jnp.where(hit, 1.0, 0.0).astype(jnp.bfloat16)
+        hot[k, :width] = hit
+        hot[k, width:] = hit
+
+    def update(c, mid, below, above):
+        value = coef[c, 0] * mid
+        if below is not None:
+            value = value + coef[c, 1] * below
+        if above is not None:
+            value = value + coef[c, 2] * above
         return (
-            coef[c, 0] * mid
-            + coef[c, 1] * src[i]
-            + coef[c, 2] * src[i + 2]
+            value
             + coef[c, 3] * pltpu.roll(mid, 1, 1)
             + coef[c, 4] * pltpu.roll(mid, width - 1, 1)
             + coef[c, 5] * pltpu.roll(mid, 1, 0)
@@ -259,60 +318,95 @@
     def other(d):
         return lax.rem(chip + d, chips) * 2 + core
 
-    def send_x(d, m):
-        slot = fc.at[mem * members + m]
-        return remote(slot, slot, x_send.at[d, m], f_recv.at[mem, m], row, other(d))
-
-    def send_p(d, m):
+    half = rows // 2
+
+    def slot(src, m, h):
+        return fc.at[src * members + m, pl.ds(h * half, half)]
+
+    def send_x(d, m, h):
+        at = slot(mem, m, h)
+        return remote(at, at, x_send.at[d, m, h], f_recv.at[mem, m, h], row, other(d))
+
+    def send_p(d, m, h):
         src = lax.rem(chip + d, chips) * 2 + core
-        slot = fc.at[src * members + m]
-        return remote(slot, slot, p_send.at[d, m], f_recv.at[src, m], row, partner)
-
-    def arrived(src, m):
-        slot = fc.at[src * members + m]
-        return remote(slot, slot, p_send.at[0, 0], f_recv.at[src, m], row, partner)
-
-    def forward(m):
+        at = slot(src, m, h)
+        return remote(at, at, p_send.at[d, m, h], f_recv.at[src, m, h], row, partner)
+
+    def arrived(src, m, h):
+        at = slot(src, m, h)
+        return remote(at, at, p_send.at[0, 0, 0], f_recv.at[src, m, h], row, partner)
+
+    def forward(m, h):
         for d in range(1, chips):
-            arrived(other(d), m).wait_recv()
-            send_p(d, m).start()
-
-    def service(m):
+            arrived(other(d), m, h).wait_recv()
+            send_p(d, m, h).start()
+
+    def give(m, h):
+        @pl.when(m > 0)
+        def _():
+            for d in range(1, chips):
+                send_x(d, m - 1, h).wait_send()
+
+        for d in range(1, chips):
+            send_x(d, m, h).start()
+        send_p(0, m, h).start()
+
+        @pl.when(m >= LAG)
+        def _():
+            forward(m - LAG, h)
+
+    def service(m, between):
+        def source(i):
+            if i < 3:
+                return hal[m, 0, i]
+            return ens[m, i - 3] if i < rows + 3 else hal[m, 1, i - rows - 3]
+
+        def steps(one, two, three):
+            for i in one:
+                w1[i] = update(i, source(i + 1), source(i), source(i + 2))
+            for i in two:
+                w2[i] = update(i + 1, w1[i + 1], w1[i], w1[i + 2])
+            for i in three:
+                fc[mem * members + m, i] = update(i + 2, w2[i + 1], w2[i], w2[i + 2])
+
         @pl.when(has_low)
         def _():
             halo_up(m).wait_recv()
-            w0[pl.ds(0, 3)] = hal[m, 0]
+
+        @pl.when(m + ahead_up < members)
+        def _():
+            send_up(m + ahead_up)
+
+        steps(range(half + 4), range(half + 2), range(half))
+        give(m, 0)
+        between()
 
         @pl.when(has_high)
         def _():
             halo_down(m).wait_recv()
-            w0[pl.ds(rows + 3, 3)] = hal[m, 1]
-
-        @pl.when(m + ahead < members)
-        def _():
-            send_halo(m + ahead)
-
-        w0[pl.ds(3, rows)] = ens[m]
-
-        @pl.loop(0, rows + 4, unroll=2)
-        def _(i):
-            w1[i] = update(w0, i, i)
-
-        @pl.loop(0, rows + 2, unroll=2)
-        def _(i):
-            w2[i] = update(w1, i, i + 1)
-
-        @pl.loop(0, rows, unroll=2)
-        def _(i):
-            fc[mem * members + m, i] = update(w2, i, i + 2)
-
-        for d in range(1, chips):
-            send_x(d, m).start()
-        send_p(0, m).start()
-
-        @pl.when(m >= LAG)
-        def _():
-            forward(m - LAG)
+
+        @pl.when(m + ahead_down < members)
+        def _():
+            send_down(m + ahead_down)
+
+        steps(range(half + 4, rows + 4), range(half + 2, rows + 2), range(half, rows))
+        give(m, 1)
+
+        @pl.when(m + DETOUR < members)
+        def _():
+            send_detour(m + DETOUR)
+
+        @pl.when(m == 0)
+        def _():
+            for n in range(FAR, RELAY):
+                relay(n)
+
+        @pl.when(m + RELAY < members)
+        def _():
+            relay(m + RELAY)
+
+    per_pass = PER_PASS if members % PER_PASS == 0 else 1
+    passes = members // per_pass
 
     inside = lax.broadcasted_iota(jnp.int32, (levels, LANES), 0)
     owner = lax.broadcasted_iota(jnp.int32, (levels, LANES), 1) // nobs
@@ -321,45 +415,56 @@
     def fold(x):
         return jnp.sum(jnp.where(pick, x, 0.0).reshape(groups, TILE, LANES), axis=1)
 
-    def profile(m):
-        z0[pl.ds(1, rows)] = ens[m]
-        z1[1] = coef[1, 2] * z0[1]
-        z1[rows + 2] = coef[rows + 2, 1] * z0[rows]
-
-        @pl.loop(0, rows, unroll=2)
-        def _(i):
-            z1[i + 2] = update(z0, i, i + 2)
-
-        z2[1] = coef[0, 2] * z1[1]
-        z2[rows + 4] = coef[rows + 3, 1] * z1[rows + 2]
-
-        @pl.loop(0, rows + 2, unroll=2)
-        def _(i):
-            z2[i + 2] = update(z1, i, i + 1)
-
-        z3[0] = cext[0] * z2[1]
-        z3[rows + 5] = cext[1] * z2[rows + 4]
-
-        @pl.loop(0, rows + 4, unroll=2)
-        def _(i):
-            z3[i + 1] = update(z2, i, i)
-
+    def profile(m, n):
+        def raw(r):
+            return ens[m, r] if 0 <= r < rows else None
+
+        def first_step(r):
+            return z1[r + 1] if -1 <= r <= rows else None
+
+        def second_step(r):
+            return z2[r + 2] if -2 <= r <= rows + 1 else None
+
+        z1[0] = coef[1, 2] * raw(0)
+        z1[rows + 1] = coef[rows + 2, 1] * raw(rows - 1)
+        for r in range(rows):
+            z1[r + 1] = update(r + 2, raw(r), raw(r - 1), raw(r + 1))
+        z2[0] = coef[0, 2] * first_step(-1)
+        z2[rows + 3] = coef[rows + 3, 1] * first_step(rows)
+        for r in range(-1, rows + 1):
+            z2[r + 2] = update(r + 2, first_step(r), first_step(r - 1), first_step(r + 1))
+
+        def split(r, x):
+            high_part = x.astype(jnp.bfloat16)
+            zb[n, r + 3, :, :width] = high_part
+            zb[n, r + 3, :, width:] = (x - high_part.astype(f32)).astype(jnp.bfloat16)
+
+        split(-3, cext[0] * second_step(-2))
+        split(rows + 2, cext[1] * second_step(rows + 1))
+        for r in range(-2, rows + 2):
+            split(r, update(r + 2, second_step(r), second_step(r - 1), second_step(r + 1)))
+
+    def extract(begin_m):
         for k, begin, count in ((0, 3, rows), (1, 0, 3), (2, rows + 3, 3)):
-            x = z3[pl.ds(begin, count)].reshape(count * levels, width)
-            high_part = x.astype(jnp.bfloat16)
-            low_part = (x - high_part.astype(f32)).astype(jnp.bfloat16)
-            got = jnp.dot(high_part, hot[k], preferred_element_type=f32)
-            got = got + jnp.dot(low_part, hot[k], preferred_element_type=f32)
+            x = zb[:, pl.ds(begin, count)].reshape(per_pass * count * levels, 2 * width)
+            got = jnp.dot(x, hot[k], preferred_element_type=f32)
             at = obsv[k, 0, :1] - row * rows + 3
-            acc = jnp.zeros((levels, LANES), f32)
-            for i in range(count):
-                acc = acc + jnp.where(at == begin + i, got[i * levels:(i + 1) * levels], 0.0)
-            pp[k, :, pl.ds(m, 1)] = fold(acc)[:, None]
+            for n in range(per_pass):
+                acc = jnp.zeros((levels, LANES), f32)
+                for i in range(count):
+                    base = (n * count + i) * levels
+                    acc = acc + jnp.where(at == begin + i, got[base:base + levels], 0.0)
+                pp[k, :, pl.ds(begin_m + n, 1)] = fold(acc)[:, None]
 
     def dot(a, b):
         return jnp.dot(a, b, precision=HIGHEST, preferred_element_type=f32)
 
     mine = pl.ds(pl.multiple_of(mem * members, members), members)
+
+    share = total // 2
+
+    def part_of(c):
+        return pl.ds(pl.multiple_of(c * share, share), share)
 
     def give_low():
         return remote(pp.at[1], prec.at[1], r_send.at[1], r_recv.at[1], low, mem)
@@ -416,13 +521,14 @@
         scal[...] = scaled
         both = jnp.concatenate([scaled, pad], axis=0)
         grec[row] = lax.dot_general(
-            scal[mine], both, (((1,), (1,)), ((), ())), precision=HIGHEST, preferred_element_type=f32
+            scal[part_of(core)], both, (((1,), (1,)), ((), ())), precision=HIGHEST, preferred_element_type=f32
         )
         for d in range(1, rows_n):
             give_gram(d).start()
 
-    def give_sum(d):
-        return remote(gall.at[mine], gall.at[mine], a_send.at[d], a_recv.at[mem], row, lax.rem(mem + d, mem_n))
+    def give_sum():
+        block = gall.at[part_of(core)]
+        return remote(block, block, a_send.at[0], a_recv.at[core], row, partner)
 
     def stage_d():
         for d in range(1, rows_n):
@@ -431,15 +537,12 @@
         part = grec[0]
         for r in range(1, rows_n):
             part = part + grec[r]
-        gall[mine] = part
-        for d in range(1, mem_n):
-            give_sum(d).start()
+        gall[part_of(core)] = part
+        give_sum().start()
 
     def stage_e():
-        for d in range(1, mem_n):
-            src = lax.rem(mem + d, mem_n)
-            block = gall.at[pl.ds(pl.multiple_of(src * members, members), members)]
-            remote(block, block, a_send.at[d], a_recv.at[src], row, src).wait_recv()
+        block = gall.at[part_of(1 - core)]
+        remote(block, block, a_send.at[0], a_recv.at[1 - core], row, partner).wait_recv()
         gsum = gall[...]
         ri = lax.broadcasted_iota(jnp.int32, (total, total), 0)
         ci = lax.broadcasted_iota(jnp.int32, (total, total), 1)
@@ -465,9 +568,9 @@
     block = min(4, members)
     tiles = width // LANES
 
-    def mix(m):
+    def mix(m, h):
         for d in range(chips):
-            arrived(lax.rem(chip + d, chips) * 2 + 1 - core, m).wait_recv()
+            arrived(lax.rem(chip + d, chips) * 2 + 1 - core, m, h).wait_recv()
 
         @pl.loop(0, members // block)
         def _(b):
@@ -479,8 +582,9 @@
                 for k in range(block)
             ]
 
-            @pl.loop(0, rows)
-            def _(i):
+            @pl.loop(0, half)
+            def _(n):
+                i = h * half + n
                 for t in range(groups):
                     for c in range(tiles):
                         at = (i, pl.ds(t * TILE, TILE), pl.ds(c * LANES, LANES))
@@ -491,41 +595,45 @@
                                 acc = acc + ws[k][s] * f[s]
                             out[(b * block + k,) + at] = acc
 
-    passes = min(4, members)
-    per_pass = cdiv(members, passes)
-    gap = max(1, (members - passes) // 6)
     at_a = passes - 1
-    at_b, at_c, at_d, at_e = (at_a + gap * n for n in range(1, 5))
-    per_mix = 3
-    mixed_in_loop = max(0, members - 1 - at_e) * per_mix
-    assert at_e < members and mixed_in_loop <= members - LAG
+    at_b, at_c, at_d, at_e = (min(at_a + n, members - 1) for n in STAGES)
+
+    def profiles(group, begin, end):
+        @pl.when(group < passes)
+        def _():
+            @pl.loop(begin, end)
+            def _(n):
+                profile(group * per_pass + n, n)
+
+            if end == per_pass:
+                extract(group * per_pass)
+
+    for k in range(3):
+        set_hot(k)
 
     @pl.loop(0, members)
     def _(m):
-        service(m)
-
-        @pl.when(m < passes)
-        def _():
-            @pl.loop(0, per_pass)
-            def _(n):
-                profile(m * per_pass + n)
+        service(m, lambda: profiles(m, 0, per_pass // 2))
+        profiles(m, per_pass // 2, per_pass)
 
         for at, stage in ((at_a, stage_a), (at_b, stage_b), (at_c, stage_c), (at_d, stage_d), (at_e, stage_e)):
             pl.when(m == at)(stage)
 
         @pl.when(m > at_e)
         def _():
-            @pl.loop(0, per_mix)
+            begin = jnp.minimum(m - LAG, (m - at_e - 1) * PER_MIX)
+            end = jnp.minimum(m - LAG + 1, (m - at_e) * PER_MIX)
+
+            @pl.loop(2 * begin, 2 * end)
             def _(n):
-                mix((m - at_e - 1) * per_mix + n)
-
-    @pl.loop(members - LAG, members)
-    def _(m):
-        forward(m)
-
-    @pl.loop(mixed_in_loop, members)
-    def _(m):
-        mix(m)
+                mix(n // 2, n % 2)
+
+    mixed_in_loop = max(0, min(members - LAG, (members - 1 - at_e) * PER_MIX))
+    late = members - LAG
+
+    @pl.loop(2 * mixed_in_loop, 2 * late)
+    def _(n):
+        mix(n // 2, n % 2)
 
     @pl.when(has_high)
     def _():
@@ -561,16 +669,43 @@
         def _():
             halo_down(m).wait_send()
 
-        for d in range(1, chips):
-            send_x(d, m).wait_send()
-        for d in range(chips):
-            send_p(d, m).wait_send()
+        @pl.when(relays(m))
+        def _():
+            relay_out(m).wait_send()
+
+        for h in range(2):
+            send_p(0, m, h).wait_send()
+
+            @pl.when(m < late)
+            def _():
+                for d in range(1, chips):
+                    send_p(d, m, h).wait_send()
 
     for d in range(1, mem_n):
         give_prof(d).wait_send()
-        give_sum(d).wait_send()
+    give_sum().wait_send()
     for d in range(1, rows_n):
         give_gram(d).wait_send()
+
+    @pl.loop(2 * late, 2 * members)
+    def _(n):
+        forward(n // 2, n % 2)
+
+        @pl.when(n > 2 * late)
+        def _():
+            mix((n - 1) // 2, (n - 1) % 2)
+
+    mix(members - 1, 1)
+
+    @pl.loop(0, LAG)
+    def _(n):
+        for h in range(2):
+            for d in range(1, chips):
+                send_p(d, late + n, h).wait_send()
+
+    for h in range(2):
+        for d in range(1, chips):
+            send_x(d, members - 1, h).wait_send()
 
 
 def per_device(rows_n, mem_n, ensemble, courant, obs_column, obs_value, obs_var):
@@ -598,33 +733,32 @@
             pltpu.VMEM((members, 2, 3) + plane, f32),
             pltpu.VMEM((rows + 4, 7) + plane, f32),
             pltpu.VMEM((2,) + plane, f32),
-            pltpu.VMEM((rows + 6,) + plane, f32),
             pltpu.VMEM((rows + 4,) + plane, f32),
             pltpu.VMEM((rows + 2,) + plane, f32),
             pltpu.VMEM((rows + 2,) + plane, f32),
             pltpu.VMEM((rows + 4,) + plane, f32),
-            pltpu.VMEM((rows + 6,) + plane, f32),
-            pltpu.VMEM((rows + 6,) + plane, f32),
+            pltpu.VMEM((PER_PASS, rows + 6, levels, 2 * width), jnp.bfloat16),
+            pltpu.VMEM((members, 3) + plane, f32),
             pltpu.VMEM((total, rows) + plane, f32),
             pltpu.VMEM((3, 2, TILE, LANES), jnp.int32),
-            pltpu.VMEM((3, width, LANES), jnp.bfloat16),
+            pltpu.VMEM((3, 2 * width, LANES), jnp.bfloat16),
             pltpu.VMEM((3, groups, members, LANES), f32),
             pltpu.VMEM((2, groups, members, LANES), f32),
             pltpu.VMEM((groups, total, LANES), f32),
             pltpu.VMEM((total, groups * LANES), f32),
-            pltpu.VMEM((rows_n, members, LANES), f32),
+            pltpu.VMEM((rows_n, total // 2, LANES), f32),
             pltpu.VMEM((total, LANES), f32),
             pltpu.VMEM((total, total), f32),
             pltpu.VMEM((members, total, LANES), f32),
             dma((members,)), dma((1,)),
             dma((2,)), dma((2,)), dma((2,)), dma((2,)),
             dma((2,)), dma((2,)), dma((2,)), dma((2,)), dma((2,)), dma((2,)),
-            dma((2, members)), dma((2, members)),
-            dma((chips, members)), dma((chips, members)), dma((mem_n, members)),
+            dma((2, members)), dma((2, members)), dma((members,)), dma((members,)),
+            dma((chips, members, 2)), dma((chips, members, 2)), dma((mem_n, members, 2)),
             dma((2,)), dma((2,)),
             dma((mem_n,)), dma((mem_n,)),
             dma((rows_n,)), dma((rows_n,)),
-            dma((mem_n,)), dma((mem_n,)),
+            dma((1,)), dma((2,)),
         ],
         compiler_params=pltpu.CompilerParams(
             collective_id=0, has_side_effects=True, vmem_limit_bytes=52 * 1024 * 1024

time: 159 us -> 135 us (0.85)
  the two profiles are of different devices: /device:TPU:8 before, /device:TPU:25 now
where the time goes in v2:
time: 135 us
  Pallas kernels  133 us (99%)
  local copies, waits for them, and re-layouts  2.19 us (2%)
    pallas_call x1, Pallas kernels, per_device(): pl.pallas_call(functools.partial(kernel, rows_n, mem_n), out_shape=pltpu....  133 us

profile of v2, /device:TPU:25, one launch (start us, length us, event | category | flops | bytes accessed | tf_op | source)
XLA Modules:
  0.0 134.9 jit_solution(1299581664968939956)
XLA Ops:
  0.0 132.7 %shard_map.55 = f32[16,6,32,384]{3,2,1,0:T(8,128)S(1)} custom-call(f32[16,6,32,384]{3,2,1,0:T(8,128)} %bitcast.6, f32[3,6,32,384]{3,2,1,0:T(8,128)} %bitcast.7, s32[16]{0:T(128)} %obs.1, f32[16,32]{1,0:T(8,128)} %bitcast.8, f32[16,32]{1,0:T(8,128)} %bitcast.9), custom_call_target="tpu_custom_call" | custom-call | tf_op jit(solution)/shard_map/pallas_call | solution.py:723
  132.7 2.2 %copy.7 = f32[16,32,6,384]{3,1,2,0:T(8,128)} copy(f32[16,32,6,384]{3,1,2,0:T(8,128)S(1)} %bitcast.5) | data formatting | bytes 9437184

commit v3 on v2

--- a/solution.py
+++ b/solution.py
@@ -32,7 +32,7 @@
     e_load, c_load,
     c_send, c_recv, cf_send, cf_recv, d_send, d_recv, df_send, df_recv, o_send, o_recv,
     h_send, h_recv, rb_recv, rf_send,
-    x_send, p_send, f_recv, r_send, r_recv, q_send, q_recv, g_send, g_recv, a_send, a_recv,
+    x_send, x_recv, p_send, p_recv, r_send, r_recv, q_send, q_recv, g_send, g_recv, a_send, a_recv,
 ):
     members, rows, levels, width = ens.shape
     total = members * mem_n
@@ -55,14 +55,16 @@
     def load_cour():
         return pltpu.make_async_copy(cour_any, cour, c_load.at[0])
 
-    def load_ens(m):
-        return pltpu.make_async_copy(ens_any.at[m], ens.at[m], e_load.at[m])
+    def load_first():
+        return pltpu.make_async_copy(ens_any.at[0], ens.at[0], e_load.at[0])
+
+    def load_rest():
+        rest = pl.ds(1, members - 1)
+        return pltpu.make_async_copy(ens_any.at[rest], ens.at[rest], e_load.at[1])
 
     load_cour().start()
-
-    @pl.loop(0, members)
-    def _(m):
-        load_ens(m).start()
+    load_first().start()
+    load_rest().start()
 
     barrier = pltpu.get_barrier_semaphore()
     for d in range(1, mem_n):
@@ -87,7 +89,7 @@
     obsv[0, 1] = oy
 
     load_cour().wait()
-    load_ens(0).wait()
+    load_first().wait()
     pl.semaphore_wait(barrier, mem_n - 1 + rows_n - 1)
 
     def chalo_up():
@@ -115,10 +117,10 @@
         return remote(obsv.at[0], obsv.at[2], o_send.at[1], o_recv.at[1], low, mem)
 
     def halo_up(m):
-        return remote(ens.at[m, pl.ds(rows - 3, 3)], hal.at[m, 0], h_send.at[0, m], h_recv.at[0, m], high, mem)
+        return remote(ens.at[m, pl.ds(rows - 3, 3)], hal.at[m, 0], h_send.at[0], h_recv.at[0, m], high, mem)
 
     def halo_down(m):
-        return remote(ens.at[m, pl.ds(0, 3)], hal.at[m, 1], h_send.at[1, m], h_recv.at[1, m], low, mem)
+        return remote(ens.at[m, pl.ds(0, 3)], hal.at[m, 1], h_send.at[1], h_recv.at[1, m], low, mem)
 
     first = core == 0
 
@@ -150,11 +152,11 @@
     def send_detour(m):
         @pl.when(jnp.logical_and(odd, detour(m)))
         def _():
-            remote(ens.at[m, pl.ds(rows - 3, 3)], rbuf.at[m], h_send.at[0, m], rb_recv.at[m], low, mem).start()
+            remote(ens.at[m, pl.ds(rows - 3, 3)], rbuf.at[m], h_send.at[0], rb_recv.at[m], low, mem).start()
 
         @pl.when(jnp.logical_and(jnp.logical_not(odd), detour(m)))
         def _():
-            remote(ens.at[m, pl.ds(0, 3)], rbuf.at[m], h_send.at[1, m], rb_recv.at[m], high, mem).start()
+            remote(ens.at[m, pl.ds(0, 3)], rbuf.at[m], h_send.at[1], rb_recv.at[m], high, mem).start()
 
     def relays(m):
         return jnp.logical_and(lax.rem(m, pairs) > relay_limit, relay_on)
@@ -190,9 +192,7 @@
 
         obs_down().start()
 
-    @pl.loop(1, members)
-    def _(m):
-        load_ens(m).wait()
+    load_rest().wait()
 
     def start_halos(near):
         @pl.when(odd == near)
@@ -323,22 +323,35 @@
     def slot(src, m, h):
         return fc.at[src * members + m, pl.ds(h * half, half)]
 
+    late = members - LAG
+
     def send_x(d, m, h):
         at = slot(mem, m, h)
-        return remote(at, at, x_send.at[d, m, h], f_recv.at[mem, m, h], row, other(d))
+        return remote(at, at, x_send.at[d - 1, h], x_recv.at[chips - d - 1, m, h], row, other(d))
+
+    def from_x(d, m, h):
+        at = slot(other(d), m, h)
+        return remote(at, at, x_send.at[0, 0], x_recv.at[d - 1, m, h], row, other(d))
+
+    def piece(d, m, h):
+        return jnp.where(m < late, m, late + ((m - late) * chips + d) * 2 + h)
 
     def send_p(d, m, h):
         src = lax.rem(chip + d, chips) * 2 + core
         at = slot(src, m, h)
-        return remote(at, at, p_send.at[d, m, h], f_recv.at[src, m, h], row, partner)
-
-    def arrived(src, m, h):
-        at = slot(src, m, h)
-        return remote(at, at, p_send.at[0, 0, 0], f_recv.at[src, m, h], row, partner)
+        return remote(at, at, p_send.at[min(d, 1)], p_recv.at[piece(d, m, h)], row, partner)
+
+    def from_p(d, m, h):
+        at = slot(lax.rem(chip + d, chips) * 2 + 1 - core, m, h)
+        return remote(at, at, p_send.at[0], p_recv.at[piece(d, m, h)], row, partner)
+
+    def from_p_whole(m):
+        at = fc.at[pl.ds(0, chips)]
+        return remote(at, at, p_send.at[0], p_recv.at[m], row, partner)
 
     def forward(m, h):
         for d in range(1, chips):
-            arrived(other(d), m, h).wait_recv()
+            from_x(d, m, h).wait_recv()
             send_p(d, m, h).start()
 
     def give(m, h):
@@ -483,7 +496,11 @@
 
     def give_prof(d):
         block = prof.at[:, mine]
-        return remote(block, block, q_send.at[d], q_recv.at[mem], row, lax.rem(mem + d, mem_n))
+        return remote(block, block, q_send.at[0], q_recv.at[0], row, lax.rem(mem + d, mem_n))
+
+    def all_profiles():
+        block = prof.at[:, pl.ds(0, (mem_n - 1) * members)]
+        return remote(block, block, q_send.at[0], q_recv.at[0], row, partner)
 
     def stage_b():
         @pl.when(has_low)
@@ -505,13 +522,14 @@
         return jnp.concatenate([got[q:q + 1] for q in range(groups)], axis=1)
 
     def give_gram(d):
-        return remote(grec.at[row], grec.at[row], g_send.at[d], g_recv.at[row], lax.rem(row + d, rows_n), mem)
+        return remote(grec.at[row], grec.at[row], g_send.at[0], g_recv.at[0], lax.rem(row + d, rows_n), mem)
+
+    def all_grams():
+        block = grec.at[pl.ds(0, rows_n - 1)]
+        return remote(block, block, g_send.at[0], g_recv.at[0], lax.rem(row + 1, rows_n), mem)
 
     def stage_c():
-        for d in range(1, mem_n):
-            src = lax.rem(mem + d, mem_n)
-            block = prof.at[:, pl.ds(pl.multiple_of(src * members, members), members)]
-            remote(block, block, q_send.at[d], q_recv.at[src], row, src).wait_recv()
+        all_profiles().wait_recv()
         values = jnp.concatenate([prof[q] for q in range(groups)], axis=1)
         variance = flat(obs_var)
         center = jnp.mean(values, axis=0, keepdims=True)
@@ -531,9 +549,7 @@
         return remote(block, block, a_send.at[0], a_recv.at[core], row, partner)
 
     def stage_d():
-        for d in range(1, rows_n):
-            src = lax.rem(row + d, rows_n)
-            remote(grec.at[src], grec.at[src], g_send.at[d], g_recv.at[src], src, mem).wait_recv()
+        all_grams().wait_recv()
         part = grec[0]
         for r in range(1, rows_n):
             part = part + grec[r]
@@ -569,8 +585,14 @@
     tiles = width // LANES
 
     def mix(m, h):
-        for d in range(chips):
-            arrived(lax.rem(chip + d, chips) * 2 + 1 - core, m, h).wait_recv()
+        @pl.when(jnp.logical_and(m < late, h == 0))
+        def _():
+            from_p_whole(m).wait_recv()
+
+        @pl.when(m >= late)
+        def _():
+            for d in range(chips):
+                from_p(d, m, h).wait_recv()
 
         @pl.loop(0, members // block)
         def _(b):
@@ -629,8 +651,6 @@
                 mix(n // 2, n % 2)
 
     mixed_in_loop = max(0, min(members - LAG, (members - 1 - at_e) * PER_MIX))
-    late = members - LAG
-
     @pl.loop(2 * mixed_in_loop, 2 * late)
     def _(n):
         mix(n // 2, n % 2)
@@ -641,6 +661,7 @@
         chalo_pass(1).wait_send()
         obs_up().wait_send()
         give_high().wait_send()
+        remote(rbuf, rbuf, h_send.at[0], rb_recv.at[0], high, mem).wait_send()
 
         @pl.when(first)
         def _():
@@ -653,6 +674,7 @@
         chalo_pass(0).wait_send()
         obs_down().wait_send()
         give_low().wait_send()
+        remote(rbuf, rbuf, h_send.at[1], rb_recv.at[0], low, mem).wait_send()
 
         @pl.when(first)
         def _():
@@ -661,51 +683,25 @@
 
     @pl.loop(0, members)
     def _(m):
-        @pl.when(has_high)
-        def _():
-            halo_up(m).wait_send()
-
-        @pl.when(has_low)
-        def _():
-            halo_down(m).wait_send()
-
         @pl.when(relays(m))
         def _():
             relay_out(m).wait_send()
 
-        for h in range(2):
-            send_p(0, m, h).wait_send()
-
-            @pl.when(m < late)
-            def _():
-                for d in range(1, chips):
-                    send_p(d, m, h).wait_send()
-
-    for d in range(1, mem_n):
-        give_prof(d).wait_send()
+    all_profiles().wait_send()
     give_sum().wait_send()
-    for d in range(1, rows_n):
-        give_gram(d).wait_send()
+    all_grams().wait_send()
 
     @pl.loop(2 * late, 2 * members)
     def _(n):
         forward(n // 2, n % 2)
-
-        @pl.when(n > 2 * late)
-        def _():
-            mix((n - 1) // 2, (n - 1) % 2)
-
-    mix(members - 1, 1)
-
-    @pl.loop(0, LAG)
-    def _(n):
-        for h in range(2):
-            for d in range(1, chips):
-                send_p(d, late + n, h).wait_send()
+        mix(n // 2, n % 2)
 
     for h in range(2):
         for d in range(1, chips):
             send_x(d, members - 1, h).wait_send()
+    for part, count in ((0, members), (1, (chips - 1) * members)):
+        at = fc.at[pl.ds(0, count)]
+        remote(at, at, p_send.at[part], p_recv.at[0], row, partner).wait_send()
 
 
 def per_device(rows_n, mem_n, ensemble, courant, obs_column, obs_value, obs_var):
@@ -750,14 +746,14 @@
             pltpu.VMEM((total, LANES), f32),
             pltpu.VMEM((total, total), f32),
             pltpu.VMEM((members, total, LANES), f32),
-            dma((members,)), dma((1,)),
+            dma((2,)), dma((1,)),
             dma((2,)), dma((2,)), dma((2,)), dma((2,)),
             dma((2,)), dma((2,)), dma((2,)), dma((2,)), dma((2,)), dma((2,)),
-            dma((2, members)), dma((2, members)), dma((members,)), dma((members,)),
-            dma((chips, members, 2)), dma((chips, members, 2)), dma((mem_n, members, 2)),
+            dma((2,)), dma((2, members)), dma((members,)), dma((members,)),
+            dma((chips - 1, 2)), dma((chips - 1, members, 2)), dma((2,)), dma((members - LAG + LAG * chips * 2,)),
             dma((2,)), dma((2,)),
-            dma((mem_n,)), dma((mem_n,)),
-            dma((rows_n,)), dma((rows_n,)),
+            dma((1,)), dma((1,)),
+            dma((1,)), dma((1,)),
             dma((1,)), dma((2,)),
         ],
         compiler_params=pltpu.CompilerParams(

time: 135 us -> 134 us (level)
  Pallas kernels: 133 us -> 131 us
where the time goes in v3:
time: 134 us
  Pallas kernels  131 us (98%)
  local copies, waits for them, and re-layouts  2.19 us (2%)
    pallas_call x1, Pallas kernels, per_device(): pl.pallas_call(functools.partial(kernel, rows_n, mem_n), out_shape=pltpu....  131 us

profile of v3, /device:TPU:25, one launch (start us, length us, event | category | flops | bytes accessed | tf_op | source)
XLA Modules:
  0.0 133.6 jit_solution(8319358796219216331)
XLA Ops:
  0.0 131.4 %shard_map.55 = f32[16,6,32,384]{3,2,1,0:T(8,128)S(1)} custom-call(f32[16,6,32,384]{3,2,1,0:T(8,128)} %bitcast.6, f32[3,6,32,384]{3,2,1,0:T(8,128)} %bitcast.7, s32[16]{0:T(128)} %obs.1, f32[16,32]{1,0:T(8,128)} %bitcast.8, f32[16,32]{1,0:T(8,128)} %bitcast.9), custom_call_target="tpu_custom_call" | custom-call | tf_op jit(solution)/shard_map/pallas_call | solution.py:719
  131.4 2.2 %copy.7 = f32[16,32,6,384]{3,1,2,0:T(8,128)} copy(f32[16,32,6,384]{3,1,2,0:T(8,128)S(1)} %bitcast.5) | data formatting | bytes 9437184

commit v4 on v3

--- a/solution.py
+++ b/solution.py
@@ -252,48 +252,53 @@
         obsv[2] = jnp.full((2, TILE, LANES), -1, jnp.int32)
         prec[1] = jnp.zeros((groups, members, LANES), f32)
 
-    def edge(side, present, begin):
+    def edge_in(side, present):
         @pl.when(present)
         def _():
             (chalo_down if side else chalo_up)().wait_recv()
             chalo_pass(side).start()
-            (obs_down if side else obs_up)().wait_recv()
-
+
+    def edge_more(side, present):
+        @pl.when(present)
+        def _():
             @pl.when(first)
             def _():
                 (far_down if side else far_up)().wait_recv()
                 far_pass(side).start()
 
+            (obs_down if side else obs_up)().wait_recv()
+
+    def edge_set(side, present, begin):
+        @pl.when(present)
+        def _():
+            chalo_pass(side).wait_recv()
+
+            @pl.loop(0, 2)
+            def _(i):
+                set_coef(begin + i, chalo[side, i, 0], chalo[side, i, 1], chalo[side, i, 2])
+
             @pl.when(jnp.logical_not(first))
             def _():
                 far_pass(side).wait_recv()
 
-            chalo_pass(side).wait_recv()
-
-            @pl.loop(0, 2)
-            def _(i):
-                set_coef(begin + i, chalo[side, i, 0], chalo[side, i, 1], chalo[side, i, 2])
-
             a0 = chalo3[side]
             cext[side] = DIFFUSION + (jnp.maximum(a0, 0.0) if side else -jnp.minimum(a0, 0.0))
 
     @pl.when(odd)
     def _():
-        edge(0, has_low, 0)
+        edge_in(1, has_high)
+        edge_in(0, has_low)
 
     @pl.when(jnp.logical_not(odd))
     def _():
-        edge(1, has_high, rows + 2)
+        edge_in(0, has_low)
+        edge_in(1, has_high)
 
     start_halos(False)
-
-    @pl.when(odd)
-    def _():
-        edge(1, has_high, rows + 2)
-
-    @pl.when(jnp.logical_not(odd))
-    def _():
-        edge(0, has_low, 0)
+    edge_more(0, has_low)
+    edge_more(1, has_high)
+    edge_set(0, has_low, 0)
+    edge_set(1, has_high, rows + 2)
 
     def set_hot(k):
         hit = lax.broadcasted_iota(jnp.int32, (width, LANES), 0) == obsv[k, 1, :1]
@@ -392,6 +397,16 @@
 
         steps(range(half + 4), range(half + 2), range(half))
         give(m, 0)
+
+        @pl.when(m == 0)
+        def _():
+            for n in range(FAR, RELAY):
+                relay(n)
+
+        @pl.when(m + RELAY < members)
+        def _():
+            relay(m + RELAY)
+
         between()
 
         @pl.when(has_high)
@@ -408,15 +423,6 @@
         @pl.when(m + DETOUR < members)
         def _():
             send_detour(m + DETOUR)
-
-        @pl.when(m == 0)
-        def _():
-            for n in range(FAR, RELAY):
-                relay(n)
-
-        @pl.when(m + RELAY < members)
-        def _():
-            relay(m + RELAY)
 
     per_pass = PER_PASS if members % PER_PASS == 0 else 1
     passes = members // per_pass

time: 134 us -> 132 us (0.985); the launches traced: 134 us -> 130 us
  Pallas kernels: 131 us -> 128 us
    pallas_call x1, Pallas kernels: 131 us -> 128 us  [per_device(): pl.pallas_call(functools.partial(kernel, rows_n, mem_n), out_shape=pltpu....]
where the time goes in v4:
time: 132 us; the launch traced here: 130 us
  Pallas kernels  128 us (97%)
  local copies, waits for them, and re-layouts  2.19 us (2%)
    pallas_call x1, Pallas kernels, per_device(): pl.pallas_call(functools.partial(kernel, rows_n, mem_n), out_shape=pltpu....  128 us

profile of v4, /device:TPU:25, one launch (start us, length us, event | category | flops | bytes accessed | tf_op | source)
XLA Modules:
  0.0 129.8 jit_solution(6675157236190711328)
XLA Ops:
  0.0 127.6 %shard_map.55 = f32[16,6,32,384]{3,2,1,0:T(8,128)S(1)} custom-call(f32[16,6,32,384]{3,2,1,0:T(8,128)} %bitcast.6, f32[3,6,32,384]{3,2,1,0:T(8,128)} %bitcast.7, s32[16]{0:T(128)} %obs.1, f32[16,32]{1,0:T(8,128)} %bitcast.8, f32[16,32]{1,0:T(8,128)} %bitcast.9), custom_call_target="tpu_custom_call" | custom-call | tf_op jit(solution)/shard_map/pallas_call | solution.py:725
  127.7 2.2 %copy.7 = f32[16,32,6,384]{3,1,2,0:T(8,128)} copy(f32[16,32,6,384]{3,1,2,0:T(8,128)S(1)} %bitcast.5) | data formatting | bytes 9437184
